TPU v7x, 512 devices: a whole 4x4x16 slice. The times are simulated.
512 devices in a mesh: frame: 32 (over x, z_lo), view: 16 (over y, z_hi, core).
Axes of the slice: x: 4, y: 4, z: 16 (z_hi: 2, z_lo: 8; z = z_hi * 8 + z_lo), core: 2. Of those that a mesh axis runs over, the one named last changes fastest.
Arguments:
- t_query: bfloat16 [16, 64, 64, 1024], P('view', 'frame'), may hold values from -8 to 8
- t_key: bfloat16 [16, 64, 64, 1024], P('view', 'frame'), may hold values from -8 to 8
- t_value: bfloat16 [16, 64, 64, 1024], P('view', 'frame'), may hold values from -6 to 6
- t_grad: bfloat16 [16, 64, 64, 1024], P('view', 'frame'), may hold values from -6 to 6
- v_query: bfloat16 [16, 64, 64, 1024], P('view', 'frame'), may hold values from -8 to 8
- v_key: bfloat16 [16, 64, 64, 1024], P('view', 'frame'), may hold values from -8 to 8
- v_value: bfloat16 [16, 64, 64, 1024], P('view', 'frame'), may hold values from -6 to 6
- v_grad: bfloat16 [16, 64, 64, 1024], P('view', 'frame'), may hold values from -6 to 6
Outputs:
- t_query_grad: bfloat16 [16, 64, 64, 1024], P('view', 'frame')
- t_key_grad: bfloat16 [16, 64, 64, 1024], P('view', 'frame')
- t_value_grad: bfloat16 [16, 64, 64, 1024], P('view', 'frame')
- v_query_grad: bfloat16 [16, 64, 64, 1024], P('view', 'frame')
- v_key_grad: bfloat16 [16, 64, 64, 1024], P('view', 'frame')
- v_value_grad: bfloat16 [16, 64, 64, 1024], P('view', 'frame')
All inputs are finite; a program needn't handle non-finite values.
Results may differ from a plain program's by a relative error of at most 0.0085.
Values may be sent and summed in bfloat16 or wider, within the bound.
A program may use at most 64 MiB of HBM per device.

v0:
```python
import jax
import jax.numpy as jnp
from jax import lax
from jax.sharding import PartitionSpec as P

HEADS = 16
HEAD_DIM = 64
ROWS = 8
COLS = 8


def product(form, left, right):
    return jnp.einsum(form, left, right, preferred_element_type=jnp.float32)


def attention_backward(
    query_block, key_block, value_block, grad_block, query_spec, key_spec, score_spec, key_count
):
    scaling = HEAD_DIM ** (-0.5)
    key_axes = tuple(range(-key_count, 0))
    scores = (
        product(query_spec + "," + key_spec + "->" + score_spec, query_block, key_block) * scaling
    )
    row_max = jnp.max(scores, axis=key_axes, keepdims=True)
    exponent = jnp.exp(scores - row_max)
    weights = exponent / jnp.sum(exponent, axis=key_axes, keepdims=True)
    rounded = weights.astype(jnp.bfloat16)
    value_grad = product(score_spec + "," + query_spec + "->" + key_spec, rounded, grad_block)
    grad_weights = product(query_spec + "," + key_spec + "->" + score_spec, grad_block, value_block)
    row_delta = jnp.sum(weights * grad_weights, axis=key_axes, keepdims=True)
    grad_scores = (weights * (grad_weights - row_delta)).astype(jnp.bfloat16)
    query_grad = (
        product(score_spec + "," + key_spec + "->" + query_spec, grad_scores, key_block) * scaling
    )
    key_grad = (
        product(score_spec + "," + query_spec + "->" + key_spec, grad_scores, query_block) * scaling
    )
    return (
        query_grad.astype(jnp.bfloat16),
        key_grad.astype(jnp.bfloat16),
        value_grad.astype(jnp.bfloat16),
    )


def temporal_work(pieces):
    count, frames, patch_part, width = pieces[0].shape
    split = [piece.reshape(count, frames, patch_part, HEADS, HEAD_DIM) for piece in pieces]
    grads = attention_backward(split[0], split[1], split[2], split[3], "nfphd", "ngphd", "nphfg", 1)
    merged = (
        grads[0].reshape(count, frames, patch_part, width),
        grads[1].reshape(count, frames, patch_part, width),
        grads[2].reshape(count, frames, patch_part, width),
    )
    return (
        lax.all_to_all(merged[0], "frame", split_axis=1, concat_axis=2, tiled=True),
        lax.all_to_all(merged[1], "frame", split_axis=1, concat_axis=2, tiled=True),
        lax.all_to_all(merged[2], "frame", split_axis=1, concat_axis=2, tiled=True),
    )


def per_device(t_query, t_key, t_value, t_grad, v_query, v_key, v_value, v_grad):
    temporal = temporal_work(
        (
            lax.all_to_all(t_query, "frame", split_axis=2, concat_axis=1, tiled=True),
            lax.all_to_all(t_key, "frame", split_axis=2, concat_axis=1, tiled=True),
            lax.all_to_all(t_value, "frame", split_axis=2, concat_axis=1, tiled=True),
            lax.all_to_all(t_grad, "frame", split_axis=2, concat_axis=1, tiled=True),
        )
    )
    view_local, frame_local, patches, width = v_query.shape
    units = frame_local * ROWS
    shaped = (
        v_query.reshape(view_local, units, COLS, width),
        v_key.reshape(view_local, units, COLS, width),
        v_value.reshape(view_local, units, COLS, width),
        v_grad.reshape(view_local, units, COLS, width),
    )
    moved = (
        lax.all_to_all(shaped[0], "view", split_axis=1, concat_axis=0, tiled=True),
        lax.all_to_all(shaped[1], "view", split_axis=1, concat_axis=0, tiled=True),
        lax.all_to_all(shaped[2], "view", split_axis=1, concat_axis=0, tiled=True),
        lax.all_to_all(shaped[3], "view", split_axis=1, concat_axis=0, tiled=True),
    )
    all_views, unit_part = (moved[0].shape[0], moved[0].shape[1])
    split = [piece.reshape(all_views, unit_part, COLS, HEADS, HEAD_DIM) for piece in moved]
    grads = attention_backward(
        split[0], split[1], split[2], split[3], "vuchd", "wuehd", "uhvcwe", 2
    )
    merged = (
        grads[0].reshape(all_views, unit_part, COLS, width),
        grads[1].reshape(all_views, unit_part, COLS, width),
        grads[2].reshape(all_views, unit_part, COLS, width),
    )
    returned = (
        lax.all_to_all(merged[0], "view", split_axis=0, concat_axis=1, tiled=True),
        lax.all_to_all(merged[1], "view", split_axis=0, concat_axis=1, tiled=True),
        lax.all_to_all(merged[2], "view", split_axis=0, concat_axis=1, tiled=True),
    )
    view_grads = tuple(
        (piece.reshape(view_local, frame_local, patches, width) for piece in returned)
    )
    return (temporal[0], temporal[1], temporal[2], view_grads[0], view_grads[1], view_grads[2])


def solution(mesh):
    placed = (
        P("view", "frame", None, None),
        P("view", "frame", None, None),
        P("view", "frame", None, None),
        P("view", "frame", None, None),
        P("view", "frame", None, None),
        P("view", "frame", None, None),
        P("view", "frame", None, None),
        P("view", "frame", None, None),
    )
    return jax.shard_map(
        per_device,
        mesh=mesh,
        in_specs=placed,
        out_specs=(
            P("view", "frame", None, None),
            P("view", "frame", None, None),
            P("view", "frame", None, None),
            P("view", "frame", None, None),
            P("view", "frame", None, None),
            P("view", "frame", None, None),
        ),
        check_vma=False,
    )
```

profile of v0, /device:TPU:6, one launch (start us, length us, event | category | flops | bytes accessed | tf_op | source)
XLA Modules:
  0.0 368.8 jit_solution(6798976928094849602)
XLA Ops:
  0.6 35.1 %all_to_all.177 = bf16[1,16,8,1024]{3,2,0,1:T(8,128)(2,1)S(1)} all-to-all(bf16[1,16,8,1024]{3,2,0,1:T(8,128)(2,1)} %bitcast.178), channel_id=1, replica_groups=mesh['frame'=32,'view'=16] {'view'}, dimensions={1} | all-to-all | bytes 524288 | tf_op jit(solution)/shard_map/all_to_all | solution.py:79
  35.7 28.6 %all_to_all.178 = bf16[1,16,8,1024]{3,2,0,1:T(8,128)(2,1)S(1)} all-to-all(bf16[1,16,8,1024]{3,2,0,1:T(8,128)(2,1)} %bitcast.179), channel_id=1, replica_groups=mesh['frame'=32,'view'=16] {'view'}, dimensions={1} | all-to-all | bytes 524288 | tf_op jit(solution)/shard_map/all_to_all | solution.py:80
  64.4 20.5 %all_to_all.179 = bf16[1,16,8,1024]{3,2,0,1:T(8,128)(2,1)S(1)} all-to-all(bf16[1,16,8,1024]{3,2,0,1:T(8,128)(2,1)} %bitcast.180), channel_id=1, replica_groups=mesh['frame'=32,'view'=16] {'view'}, dimensions={1} | all-to-all | bytes 524288 | tf_op jit(solution)/shard_map/all_to_all | solution.py:82
  90.4 15.0 %all-to-all-done.10 = bf16[1,16,8,1024]{3,2,0,1:T(8,128)(2,1)S(1)} async-done(((bf16[1,16,8,1024]{3,2,0,1:T(8,128)(2,1)}), bf16[1,16,8,1024]{3,2,0,1:T(8,128)(2,1)S(1)}, u32[]{:S(2)}, u32[]{:S(2)}) %all-to-all-start.10) | async-done | bytes 262176 | tf_op jit(solution)/shard_map/all_to_all | solution.py:81
  105.4 18.5 %all-to-all-start = ((bf16[1,2,64,1024]{3,1,0,2:T(2,128)(2,1)}), bf16[1,2,64,1024]{3,1,0,2:T(2,128)(2,1)S(1)}, u32[]{:S(2)}, u32[]{:S(2)}) async-start(bf16[1,2,64,1024]{3,1,0,2:T(2,128)(2,1)} %copy.90), calls=%async_computation | async-start | bytes 524288 | tf_op jit(solution)/shard_map/all_to_all | solution.py:64
  125.8 15.6 %all-to-all-done = bf16[1,2,64,1024]{3,1,0,2:T(2,128)(2,1)S(1)} async-done(((bf16[1,2,64,1024]{3,1,0,2:T(2,128)(2,1)}), bf16[1,2,64,1024]{3,1,0,2:T(2,128)(2,1)S(1)}, u32[]{:S(2)}, u32[]{:S(2)}) %all-to-all-start) | async-done | bytes 262176 | tf_op jit(solution)/shard_map/all_to_all | solution.py:64
  141.4 7.4 %all-to-all-start.1 = ((bf16[1,2,64,1024]{3,1,0,2:T(2,128)(2,1)}), bf16[1,2,64,1024]{3,1,0,2:T(2,128)(2,1)S(1)}, u32[]{:S(2)}, u32[]{:S(2)}) async-start(bf16[1,2,64,1024]{3,1,0,2:T(2,128)(2,1)} %copy.92), calls=%async_computation.1 | async-start | bytes 524288 | tf_op jit(solution)/shard_map/all_to_all | solution.py:65
  165.5 9.9 %all-to-all-start.2 = ((bf16[1,2,64,1024]{3,1,0,2:T(2,128)(2,1)}), bf16[1,2,64,1024]{3,1,0,2:T(2,128)(2,1)S(1)}, u32[]{:S(2)}, u32[]{:S(2)}) async-start(bf16[1,2,64,1024]{3,1,0,2:T(2,128)(2,1)} %copy.96), calls=%async_computation.2 | async-start | bytes 524288 | tf_op jit(solution)/shard_map/all_to_all | solution.py:67
  175.4 7.9 %multiply_reduce_fusion = (f32[16,16,8]{1,2,0:T(8,128)S(1)}, f32[16,16,8,16,8]{1,3,4,2,0:T(8,128)}) fusion(f32[16,16,8]{1,2,0:T(8,128)S(1)} %fusion.2, f32[16,16,8]{1,2,0:T(8,128)S(1)} %get-tuple-element.22, f32[16,16,8,16,8]{1,3,4,2,0:T(8,128)} %copy-done, bf16[16,8,16,64,1]{3,2,1,0,4:T(8,128)(2,1)} %bitcast.177, bf16[16,8,16,64,1]{3,2,1,0,4:T(8,128)(2,1)S(1)} %bitcast.175), kind=kOutput, calls=%fused_computation.2 | convolution fusion | flops 34863104 | bytes 2646016 | tf_op jit(solution)/shard_map/vuchd,wuehd->uhvcwe/dot_general | solution.py:13
  183.2 8.3 %all-to-all-done.2 = bf16[1,2,64,1024]{3,1,0,2:T(2,128)(2,1)S(1)} async-done(((bf16[1,2,64,1024]{3,1,0,2:T(2,128)(2,1)}), bf16[1,2,64,1024]{3,1,0,2:T(2,128)(2,1)S(1)}, u32[]{:S(2)}, u32[]{:S(2)}) %all-to-all-start.2) | async-done | bytes 262176 | tf_op jit(solution)/shard_map/all_to_all | solution.py:67
  191.5 7.5 %all-to-all-start.3 = ((bf16[1,2,64,1024]{3,1,0,2:T(2,128)(2,1)}), bf16[1,2,64,1024]{3,1,0,2:T(2,128)(2,1)S(1)}, u32[]{:S(2)}, u32[]{:S(2)}) async-start(bf16[1,2,64,1024]{3,1,0,2:T(2,128)(2,1)} %copy.98), calls=%async_computation.3 | async-start | bytes 524288 | tf_op jit(solution)/shard_map/all_to_all | solution.py:66
  199.0 7.3 %multiply_convert_fusion = bf16[16,16,8,16,8]{1,3,4,2,0:T(8,128)(2,1)S(1)} fusion(f32[16,16,8,16,8]{1,3,4,2,0:T(8,128)} %get-tuple-element.25, f32[16,16,8]{1,2,0:T(8,128)S(1)} %get-tuple-element.24, f32[16,16,8]{1,2,0:T(8,128)S(1)} %fusion.2, f32[16,16,8]{1,2,0:T(8,128)S(1)} %get-tuple-element.22, f32[16,16,8,16,8]{1,3,4,2,0:T(8,128)} %copy-done), kind=kLoop, calls=%fused_computation.1 | loop fusion | flops 1572864 | bytes 2646016 | tf_op jit(solution)/shard_map/convert_element_type | solution.py:31
  211.2 4.1 %all-to-all-done.3 = bf16[1,2,64,1024]{3,1,0,2:T(2,128)(2,1)S(1)} async-done(((bf16[1,2,64,1024]{3,1,0,2:T(2,128)(2,1)}), bf16[1,2,64,1024]{3,1,0,2:T(2,128)(2,1)S(1)}, u32[]{:S(2)}, u32[]{:S(2)}) %all-to-all-start.3) | async-done | bytes 262176 | tf_op jit(solution)/shard_map/all_to_all | solution.py:66
  223.9 12.1 %all-to-all-done.12 = bf16[16,1,8,1024]{3,2,1,0:T(8,128)(2,1)S(1)} async-done(((bf16[16,1,8,1024]{3,2,1,0:T(8,128)(2,1)}), bf16[16,1,8,1024]{3,2,1,0:T(8,128)(2,1)S(1)}, u32[]{:S(2)}, u32[]{:S(2)}) %all-to-all-start.12) | async-done | bytes 262176 | tf_op jit(solution)/shard_map/all_to_all | solution.py:96
  239.5 5.8 %fusion.21 = bf16[16,1,8,16,64]{4,0,2,3,1:T(8,128)(2,1)S(1)} fusion(bf16[16,8,16,64,1]{3,2,1,0,4:T(8,128)(2,1)S(1)} %bitcast.176, f32[16,16,8,16,8]{1,3,4,2,0:T(8,128)} %copy-done, f32[16,16,8]{1,2,0:T(8,128)S(1)} %fusion.2, f32[16,16,8]{1,2,0:T(8,128)S(1)} %get-tuple-element.22), kind=kOutput, calls=%fused_computation.27 | convolution fusion | flops 34734080 | bytes 1589248 | tf_op jit(solution)/shard_map/uhvcwe,vuchd->wuehd/dot_general | solution.py:13
  247.8 8.7 %all-to-all-done.11 = bf16[16,1,8,1024]{3,2,1,0:T(8,128)(2,1)S(1)} async-done(((bf16[16,1,8,1024]{3,2,1,0:T(8,128)(2,1)}), bf16[16,1,8,1024]{3,2,1,0:T(8,128)(2,1)S(1)}, u32[]{:S(2)}, u32[]{:S(2)}) %all-to-all-start.11) | async-done | bytes 262176 | tf_op jit(solution)/shard_map/all_to_all | solution.py:95
  256.4 8.9 %all-to-all-start.13 = ((bf16[16,1,8,1024]{3,2,1,0:T(8,128)(2,1)}), bf16[16,1,8,1024]{3,2,1,0:T(8,128)(2,1)S(1)}, u32[]{:S(2)}, u32[]{:S(2)}) async-start(bf16[16,1,8,1024]{3,2,1,0:T(8,128)(2,1)} %bitcast.58), calls=%async_computation.13 | async-start | bytes 524288 | tf_op jit(solution)/shard_map/all_to_all | solution.py:97
  272.8 9.5 %all-to-all-done.13 = bf16[16,1,8,1024]{3,2,1,0:T(8,128)(2,1)S(1)} async-done(((bf16[16,1,8,1024]{3,2,1,0:T(8,128)(2,1)}), bf16[16,1,8,1024]{3,2,1,0:T(8,128)(2,1)S(1)}, u32[]{:S(2)}, u32[]{:S(2)}) %all-to-all-start.13) | async-done | bytes 262176 | tf_op jit(solution)/shard_map/all_to_all | solution.py:97
  282.3 17.8 %all-to-all-start.5 = ((bf16[1,64,2,1024]{3,2,0,1:T(2,128)(2,1)}), bf16[1,64,2,1024]{3,2,0,1:T(2,128)(2,1)S(1)}, u32[]{:S(2)}, u32[]{:S(2)}) async-start(bf16[1,64,2,1024]{3,2,0,1:T(2,128)(2,1)} %copy.109), calls=%async_computation.5 | async-start | bytes 524288 | tf_op jit(solution)/shard_map/all_to_all | solution.py:56
  301.4 16.2 %all-to-all-done.5 = bf16[1,64,2,1024]{3,2,0,1:T(2,128)(2,1)S(1)} async-done(((bf16[1,64,2,1024]{3,2,0,1:T(2,128)(2,1)}), bf16[1,64,2,1024]{3,2,0,1:T(2,128)(2,1)S(1)}, u32[]{:S(2)}, u32[]{:S(2)}) %all-to-all-start.5) | async-done | bytes 262176 | tf_op jit(solution)/shard_map/all_to_all | solution.py:56
  317.6 7.4 %all-to-all-start.4 = ((bf16[1,64,2,1024]{3,2,0,1:T(2,128)(2,1)}), bf16[1,64,2,1024]{3,2,0,1:T(2,128)(2,1)S(1)}, u32[]{:S(2)}, u32[]{:S(2)}) async-start(bf16[1,64,2,1024]{3,2,0,1:T(2,128)(2,1)} %copy.105), calls=%async_computation.4 | async-start | bytes 524288 | tf_op jit(solution)/shard_map/all_to_all | solution.py:55
  328.1 13.6 %all-to-all-done.4 = bf16[1,64,2,1024]{3,2,0,1:T(2,128)(2,1)S(1)} async-done(((bf16[1,64,2,1024]{3,2,0,1:T(2,128)(2,1)}), bf16[1,64,2,1024]{3,2,0,1:T(2,128)(2,1)S(1)}, u32[]{:S(2)}, u32[]{:S(2)}) %all-to-all-start.4) | async-done | bytes 262176 | tf_op jit(solution)/shard_map/all_to_all | solution.py:55
  341.7 7.4 %all-to-all-start.6 = ((bf16[1,64,2,1024]{3,2,0,1:T(2,128)(2,1)}), bf16[1,64,2,1024]{3,2,0,1:T(2,128)(2,1)S(1)}, u32[]{:S(2)}, u32[]{:S(2)}) async-start(bf16[1,64,2,1024]{3,2,0,1:T(2,128)(2,1)} %reshape.250), calls=%async_computation.6 | async-start | bytes 524288 | tf_op jit(solution)/shard_map/all_to_all | solution.py:57
  351.1 14.6 %all-to-all-done.6 = bf16[1,64,2,1024]{3,2,0,1:T(2,128)(2,1)S(1)} async-done(((bf16[1,64,2,1024]{3,2,0,1:T(2,128)(2,1)}), bf16[1,64,2,1024]{3,2,0,1:T(2,128)(2,1)S(1)}, u32[]{:S(2)}, u32[]{:S(2)}) %all-to-all-start.6) | async-done | bytes 262176 | tf_op jit(solution)/shard_map/all_to_all | solution.py:57
  (55 shorter events, 60.1 us)
Async XLA Ops:
  84.9 20.5 %all-to-all-start.10 = ((bf16[1,16,8,1024]{3,2,0,1:T(8,128)(2,1)}), bf16[1,16,8,1024]{3,2,0,1:T(8,128)(2,1)S(1)}, u32[]{:S(2)}, u32[]{:S(2)}) async-start(bf16[1,16,8,1024]{3,2,0,1:T(8,128)(2,1)} %bitcast.181), calls=%async_computation.10 | async-start | bytes 524288 | tf_op jit(solution)/shard_map/all_to_all | solution.py:81
  105.4 36.0 %all-to-all-start = ((bf16[1,2,64,1024]{3,1,0,2:T(2,128)(2,1)}), bf16[1,2,64,1024]{3,1,0,2:T(2,128)(2,1)S(1)}, u32[]{:S(2)}, u32[]{:S(2)}) async-start(bf16[1,2,64,1024]{3,1,0,2:T(2,128)(2,1)} %copy.90), calls=%async_computation | async-start | bytes 524288 | tf_op jit(solution)/shard_map/all_to_all | solution.py:64
  141.4 24.1 %all-to-all-start.1 = ((bf16[1,2,64,1024]{3,1,0,2:T(2,128)(2,1)}), bf16[1,2,64,1024]{3,1,0,2:T(2,128)(2,1)S(1)}, u32[]{:S(2)}, u32[]{:S(2)}) async-start(bf16[1,2,64,1024]{3,1,0,2:T(2,128)(2,1)} %copy.92), calls=%async_computation.1 | async-start | bytes 524288 | tf_op jit(solution)/shard_map/all_to_all | solution.py:65
  157.2 3.2 copy-start
  165.5 26.0 %all-to-all-start.2 = ((bf16[1,2,64,1024]{3,1,0,2:T(2,128)(2,1)}), bf16[1,2,64,1024]{3,1,0,2:T(2,128)(2,1)S(1)}, u32[]{:S(2)}, u32[]{:S(2)}) async-start(bf16[1,2,64,1024]{3,1,0,2:T(2,128)(2,1)} %copy.96), calls=%async_computation.2 | async-start | bytes 524288 | tf_op jit(solution)/shard_map/all_to_all | solution.py:67
  191.5 23.8 %all-to-all-start.3 = ((bf16[1,2,64,1024]{3,1,0,2:T(2,128)(2,1)}), bf16[1,2,64,1024]{3,1,0,2:T(2,128)(2,1)S(1)}, u32[]{:S(2)}, u32[]{:S(2)}) async-start(bf16[1,2,64,1024]{3,1,0,2:T(2,128)(2,1)} %copy.98), calls=%async_computation.3 | async-start | bytes 524288 | tf_op jit(solution)/shard_map/all_to_all | solution.py:66
  206.4 2.0 copy-start.1
  215.3 20.7 %all-to-all-start.12 = ((bf16[16,1,8,1024]{3,2,1,0:T(8,128)(2,1)}), bf16[16,1,8,1024]{3,2,1,0:T(8,128)(2,1)S(1)}, u32[]{:S(2)}, u32[]{:S(2)}) async-start(bf16[16,1,8,1024]{3,2,1,0:T(8,128)(2,1)} %bitcast.50), calls=%async_computation.12 | async-start | bytes 524288 | tf_op jit(solution)/shard_map/all_to_all | solution.py:96
  236.0 20.4 %all-to-all-start.11 = ((bf16[16,1,8,1024]{3,2,1,0:T(8,128)(2,1)}), bf16[16,1,8,1024]{3,2,1,0:T(8,128)(2,1)S(1)}, u32[]{:S(2)}, u32[]{:S(2)}) async-start(bf16[16,1,8,1024]{3,2,1,0:T(8,128)(2,1)} %bitcast.42), calls=%async_computation.11 | async-start | bytes 524288 | tf_op jit(solution)/shard_map/all_to_all | solution.py:95
  256.4 25.8 %all-to-all-start.13 = ((bf16[16,1,8,1024]{3,2,1,0:T(8,128)(2,1)}), bf16[16,1,8,1024]{3,2,1,0:T(8,128)(2,1)S(1)}, u32[]{:S(2)}, u32[]{:S(2)}) async-start(bf16[16,1,8,1024]{3,2,1,0:T(8,128)(2,1)} %bitcast.58), calls=%async_computation.13 | async-start | bytes 524288 | tf_op jit(solution)/shard_map/all_to_all | solution.py:97
  267.5 2.3 copy-start.2
  282.3 35.3 %all-to-all-start.5 = ((bf16[1,64,2,1024]{3,2,0,1:T(2,128)(2,1)}), bf16[1,64,2,1024]{3,2,0,1:T(2,128)(2,1)S(1)}, u32[]{:S(2)}, u32[]{:S(2)}) async-start(bf16[1,64,2,1024]{3,2,0,1:T(2,128)(2,1)} %copy.109), calls=%async_computation.5 | async-start | bytes 524288 | tf_op jit(solution)/shard_map/all_to_all | solution.py:56
  317.6 24.1 %all-to-all-start.4 = ((bf16[1,64,2,1024]{3,2,0,1:T(2,128)(2,1)}), bf16[1,64,2,1024]{3,2,0,1:T(2,128)(2,1)S(1)}, u32[]{:S(2)}, u32[]{:S(2)}) async-start(bf16[1,64,2,1024]{3,2,0,1:T(2,128)(2,1)} %copy.105), calls=%async_computation.4 | async-start | bytes 524288 | tf_op jit(solution)/shard_map/all_to_all | solution.py:55
  341.7 24.0 %all-to-all-start.6 = ((bf16[1,64,2,1024]{3,2,0,1:T(2,128)(2,1)}), bf16[1,64,2,1024]{3,2,0,1:T(2,128)(2,1)S(1)}, u32[]{:S(2)}, u32[]{:S(2)}) async-start(bf16[1,64,2,1024]{3,2,0,1:T(2,128)(2,1)} %reshape.250), calls=%async_computation.6 | async-start | bytes 524288 | tf_op jit(solution)/shard_map/all_to_all | solution.py:57
where the time goes:
time: 372 us; the launch traced here: 369 us
  waiting for transfers between devices  120 us (32%)
  starting transfers between devices  95.4 us (26%)
  blocking collectives  84.3 us (23%)
  local copies, waits for them, and re-layouts  29.6 us (8%)
  matrix products  26.9 us (7%)
  other arithmetic  11.3 us (3%)
    all_to_all x1, blocking collectives, per_device(): lax.all_to_all(shaped[0], 'view', split_axis=1, concat_axis=0, tiled=True)  35.1 us
    all_to_all x1, blocking collectives, per_device(): lax.all_to_all(shaped[1], 'view', split_axis=1, concat_axis=0, tiled=True)  28.6 us
    dot_general x9, matrix products, product(): return jnp.einsum(form, left, right, preferred_element_type=jnp.float32)  25.3 us
    all_to_all x1, blocking collectives, per_device(): lax.all_to_all(shaped[3], 'view', split_axis=1, concat_axis=0, tiled=True)  20.5 us
    all_to_all x1, starting transfers between devices, per_device(): lax.all_to_all(t_query, 'frame', split_axis=2, concat_axis=1, tiled=True)  18.5 us
    all_to_all x1, starting transfers between devices, temporal_work(): lax.all_to_all(merged[1], 'frame', split_axis=1, concat_axis=2, tiled=True)  17.8 us
    unnamed x16, local copies, waits for them, and re-layouts  17.2 us
    all_to_all x1, waiting for transfers between devices, temporal_work(): lax.all_to_all(merged[1], 'frame', split_axis=1, concat_axis=2, tiled=True)  16.2 us
  transfers between devices with their start and end apart: 11, of which 11 were waited for; matrix products, arithmetic and copies ran while one was open for 16% of the time, Pallas kernels for 0%

commit v1 on v0

v1 whole, which is shorter than its diff:
```python
import functools

import jax
import jax.numpy as jnp
from jax import lax
from jax.experimental import pallas as pl
from jax.experimental.pallas import tpu as pltpu
from jax.sharding import PartitionSpec as P

MESH = pl.DeviceIdType.MESH
HEAD_DIM = 64
LANES = 256
HALF = 128
GROUP = LANES // HEAD_DIM
ROW = 8
F32 = jnp.float32
BF16 = jnp.bfloat16


def flip(index, mask, bits):
    total = 0
    for bit in range(bits):
        width = 1 << bit
        one = lax.rem(lax.div(index, width), 2)
        two = lax.rem(lax.div(mask, width), 2)
        total = total + (one + two - 2 * one * two) * width
    return total


def dot(left, right, left_axis, right_axis):
    return lax.dot_general(
        left, right, (((left_axis,), (right_axis,)), ((), ())), preferred_element_type=F32
    )


def masks(rows, dtype):
    lane = lax.broadcasted_iota(jnp.int32, (rows, LANES), 1)
    return [
        jnp.where((lane >= h * HEAD_DIM) & (lane < (h + 1) * HEAD_DIM), 1.0, 0.0).astype(dtype)
        for h in range(GROUP)
    ]


def attention(query, key, value, grad):
    rows = query.shape[0]
    scaling = HEAD_DIM ** (-0.5)
    narrow, wide = masks(rows, BF16), masks(rows, F32)
    queries = jnp.concatenate([query * m for m in narrow], axis=0)
    grads = jnp.concatenate([grad * m for m in narrow], axis=0)
    scores = dot(key, queries, 1, 1) * scaling
    exponent = jnp.exp(scores - jnp.max(scores, axis=0, keepdims=True))
    weights = exponent / jnp.sum(exponent, axis=0, keepdims=True)
    grad_weights = dot(value, grads, 1, 1)
    delta = jnp.sum(weights * grad_weights, axis=0, keepdims=True)
    grad_scores = (weights * (grad_weights - delta)).astype(BF16)
    value_grad = dot(weights.astype(BF16), grads, 1, 0)
    key_grad = dot(grad_scores, queries, 1, 0) * scaling
    spread = dot(grad_scores, key, 0, 0)
    query_grad = spread[:rows] * wide[0]
    for h in range(1, GROUP):
        query_grad = query_grad + spread[h * rows : (h + 1) * rows] * wide[h]
    return query_grad * scaling, key_grad, value_grad


def kernel(frames, views, *refs):
    t_in, v_in, t_out, v_out = refs[:4], refs[4:8], refs[8:11], refs[11:14]
    t_got, v_got, t_made, v_made, t_wide, o_wide, send, recv = refs[14:]
    frame, view = lax.axis_index("frame"), lax.axis_index("view")
    local = 2
    frame_bits, view_bits = frames.bit_length() - 1, views.bit_length() - 1
    lane_groups = 1024 // LANES

    barrier = pltpu.get_barrier_semaphore()

    def greet_view(k, _):
        pl.semaphore_signal(
            barrier, inc=1, device_id=(frame, flip(view, k, view_bits)), device_id_type=MESH
        )
        return 0

    def greet_frame(k, _):
        pl.semaphore_signal(
            barrier, inc=1, device_id=(flip(frame, k, frame_bits), view), device_id_type=MESH
        )
        return 0

    lax.fori_loop(1, views, greet_view, 0)
    lax.fori_loop(1, frames, greet_frame, 0)
    pl.semaphore_wait(barrier, views + frames - 2)

    def unit(ref, index):
        row = pl.multiple_of(lax.rem(index, 8) * ROW, ROW)
        return ref.at[lax.div(index, 8), pl.ds(row, ROW), :]

    def part(ref, index):
        row = pl.multiple_of(lax.div(index, lane_groups) * ROW, ROW)
        lane = pl.multiple_of(lax.rem(index, lane_groups) * LANES, LANES)
        return ref.at[:, pl.ds(row, ROW), pl.ds(lane, LANES)]

    def own_frames(ref, index):
        return ref.at[pl.ds(index * local, local)]

    def exchange(count, bits, axis, sources, targets, take, put, first):
        me = frame if axis == "frame" else view

        def step(k, _):
            peer = flip(me, k, bits)
            where = (peer, view) if axis == "frame" else (frame, peer)
            for i, (source, target) in enumerate(zip(sources, targets)):
                pltpu.make_async_remote_copy(
                    src_ref=take(source, peer),
                    dst_ref=put(target, me),
                    send_sem=send.at[first + i],
                    recv_sem=recv.at[first + i],
                    device_id=where,
                    device_id_type=MESH,
                ).start()
            return 0

        for i, (source, target) in enumerate(zip(sources, targets)):
            pltpu.make_async_copy(take(source, me), put(target, me), recv.at[first + i]).start()
        lax.fori_loop(1, count, step, 0)

    def landed(targets, first):
        for i, target in enumerate(targets):
            pltpu.make_async_copy(target, target, recv.at[first + i]).wait()

    def left(count, piece, first, number):
        for i in range(number):
            sent = piece.at[pl.ds(0, count)]
            pltpu.make_async_copy(sent, sent, send.at[first + i]).wait()

    t_into = [t_got.at[i] for i in range(4)]
    v_into = [v_got.at[i] for i in range(4)]
    t_from = [t_made.at[i] for i in range(3)]
    v_from = [v_made.at[i] for i in range(3)]

    exchange(views, view_bits, "view", v_in, v_into, unit, lambda r, i: r.at[i], 0)
    exchange(frames, frame_bits, "frame", t_in, t_into, part, own_frames, 4)

    landed(v_into, 0)
    v_rows = v_got.shape[1] * ROW

    def view_heads(j, _):
        lanes = pl.ds(pl.multiple_of(j * LANES, LANES), LANES)
        block = [v_got[i, :, :, lanes].reshape(v_rows, LANES) for i in range(4)]
        for i, value in enumerate(attention(*block)):
            v_made[i, :, :, lanes] = value.astype(BF16).reshape(v_rows // ROW, ROW, LANES)
        return 0

    lax.fori_loop(0, lane_groups, view_heads, 0)
    exchange(views, view_bits, "view", v_from, v_out, lambda r, i: r.at[i], unit, 8)

    landed(t_into, 4)
    steps = t_got.shape[1]

    def widen(j, _):
        frames_of = pl.ds(j * ROW, ROW)
        rows_of = pl.ds(pl.multiple_of(j * ROW * ROW, ROW * ROW), ROW * ROW)
        for i in range(4):
            rows = t_got[i, frames_of].astype(F32).reshape(ROW * ROW, LANES)
            t_wide[i, 0, rows_of, :] = rows[:, :HALF]
            t_wide[i, 1, rows_of, :] = rows[:, HALF:]
        return 0

    lax.fori_loop(0, steps // ROW, widen, 0)

    def patch(j, _):
        rows_of = pl.ds(j, steps, stride=ROW)
        block = [
            jnp.concatenate([t_wide[i, h, rows_of, :] for h in range(2)], axis=1).astype(BF16)
            for i in range(4)
        ]
        for i, value in enumerate(attention(*block)):
            o_wide[i, 0, rows_of, :] = value[:, :HALF]
            o_wide[i, 1, rows_of, :] = value[:, HALF:]
        return 0

    lax.fori_loop(0, ROW, patch, 0)

    def narrow(j, _):
        frames_of = pl.ds(j * ROW, ROW)
        rows_of = pl.ds(pl.multiple_of(j * ROW * ROW, ROW * ROW), ROW * ROW)
        for i in range(3):
            rows = jnp.concatenate([o_wide[i, h, rows_of, :] for h in range(2)], axis=1)
            t_made[i, frames_of] = rows.astype(BF16).reshape(ROW, ROW, LANES)
        return 0

    lax.fori_loop(0, steps // ROW, narrow, 0)
    exchange(frames, frame_bits, "frame", t_from, t_out, own_frames, part, 11)

    landed(v_out, 8)
    landed(t_out, 11)
    left(views - 1, v_got.at[0], 0, 4)
    left((frames - 1) * local, t_got.at[0], 4, 4)
    left(views - 1, v_made.at[0], 8, 3)
    left((frames - 1) * local, t_made.at[0], 11, 3)


def per_device(frames, views, *arrays):
    shape = arrays[0].shape
    flat = [array.reshape(shape[1:]) for array in arrays]
    whole = frames * shape[1]
    out = pl.pallas_call(
        functools.partial(kernel, frames, views),
        name="both_blocks",
        out_shape=[jax.ShapeDtypeStruct(shape[1:], BF16)] * 6,
        in_specs=[pl.BlockSpec(memory_space=pl.ANY)] * 8,
        out_specs=[pl.BlockSpec(memory_space=pl.ANY)] * 6,
        scratch_shapes=[
            pltpu.VMEM((4, whole, ROW, LANES), BF16),
            pltpu.VMEM((4, views, ROW, shape[3]), BF16),
            pltpu.VMEM((3, whole, ROW, LANES), BF16),
            pltpu.VMEM((3, views, ROW, shape[3]), BF16),
            pltpu.VMEM((4, 2, whole * ROW, HALF), F32),
            pltpu.VMEM((3, 2, whole * ROW, HALF), F32),
            pltpu.SemaphoreType.DMA((14,)),
            pltpu.SemaphoreType.DMA((14,)),
        ],
        compiler_params=pltpu.CompilerParams(collective_id=0, has_side_effects=True),
    )(*flat)
    return tuple(array.reshape(shape) for array in out)


def solution(mesh):
    placed = P("view", "frame", None, None)
    return jax.shard_map(
        functools.partial(per_device, mesh.shape["frame"], mesh.shape["view"]),
        mesh=mesh,
        in_specs=(placed,) * 8,
        out_specs=(placed,) * 6,
        check_vma=False,
    )
```

time: 372 us -> 195 us (0.52)
  Pallas kernels: 0 us -> 188 us
  waiting for transfers between devices: 120 us -> 0 us
  starting transfers between devices: 95.4 us -> 0 us
  blocking collectives: 84.3 us -> 0 us
  matrix products: 26.9 us -> 0 us
  local copies, waits for them, and re-layouts: 29.6 us -> 6.59 us
  other arithmetic: 11.3 us -> 0 us
    pallas_call x0 -> x1, Pallas kernels: none -> 188 us  [per_device(): pl.pallas_call(functools.partial(kernel, frames, views), name='both_block...]
    all_to_all x11 -> x0, waiting for transfers between devices: 120 us -> none  [the longest x1 16.2 us: temporal_work(): lax.all_to_all(merged[1], 'frame', split_axis=1, concat_axis=2, tiled=True)]
    all_to_all x11 -> x0, starting transfers between devices: 95.4 us -> none  [the longest x1 18.5 us: per_device(): lax.all_to_all(t_query, 'frame', split_axis=2, concat_axis=1, tiled=True)]
    all_to_all x3 -> x0, blocking collectives: 84.3 us -> none  [the longest x1 35.1 us: per_device(): lax.all_to_all(shaped[0], 'view', split_axis=1, concat_axis=0, tiled=True)]
    dot_general x9 -> x0, matrix products: 25.3 us -> none  [product(): return jnp.einsum(form, left, right, preferred_element_type=jnp.float32)]
    unnamed x16, local copies, waits for them, and re-layouts: 17.2 us -> 6.59 us
    convert_element_type x2 -> x0, other arithmetic: 8.83 us -> none  [attention_backward(): grad_scores = (weights * (grad_weights - row_delta)).astype(jnp.bfloat16)]
    reshape x7 -> x0, local copies, waits for them, and re-layouts: 6.45 us -> none  [the longest x2 1.36 us: temporal_work(): grads[2].reshape(count, frames, patch_part, width)]
  transfers between devices with their start and end apart: 11 -> 0, of which waited for: 11 -> 0; matrix products, arithmetic and copies ran while one was open for 16% -> 0% of each run, Pallas kernels for 0% -> 0%
where the time goes in v1:
time: 195 us
  Pallas kernels  188 us (96%)
  local copies, waits for them, and re-layouts  6.59 us (3%)
    pallas_call x1, Pallas kernels, per_device(): pl.pallas_call(functools.partial(kernel, frames, views), name='both_block...  188 us
    unnamed x16, local copies, waits for them, and re-layouts  6.59 us

profile of v1, /device:TPU:6, one launch (start us, length us, event | category | flops | bytes accessed | tf_op | source)
XLA Modules:
  0.0 195.0 jit_solution(5441857927568660422)
XLA Ops:
  0.6 187.8 %both_blocks.1 = (bf16[2,64,1024]{2,1,0:T(8,128)(2,1)}, bf16[2,64,1024]{2,1,0:T(8,128)(2,1)}, bf16[2,64,1024]{2,1,0:T(8,128)(2,1)}, bf16[2,64,1024]{2,1,0:T(8,12...) custom-call(bf16[2,64,1024]{2,1,0:T(8,128)(2,1)} %bitcast.20, bf16[2,64,1024]{2,1,0:T(8,128)(2,1)} %bitcast.21, ...), custom_call_target="tpu_custom_call" | custom-call | tf_op jit(solution)/shard_map/both_blocks/pallas_call | solution.py:204
  188.4 0.0 copy-start.4
  188.4 1.7 copy.20
  190.1 0.0 copy-done.4
  190.1 0.0 copy-start.3
  190.1 0.7 copy.21
  190.8 0.3 copy-done.3
  191.2 0.0 copy-start.2
  191.2 0.7 copy.22
  191.9 0.3 copy-done.2
  192.2 0.0 copy-start.1
  192.2 0.7 copy.23
  192.9 0.3 copy-done.1
  193.3 0.0 copy-start
  193.3 0.7 copy.24
  194.0 0.3 copy-done
  194.3 0.7 copy.25
Async XLA Ops:
  188.4 1.7 copy-start.4
  190.1 1.0 copy-start.3
  191.2 1.0 copy-start.2
  192.2 1.0 copy-start.1
  193.3 1.0 copy-start
